TPU v7x, 256 devices: a whole 4x4x8 slice. The times are simulated.
256 devices in a mesh: band: 16 (over y, z_lo, core), shard: 16 (over z_hi, x).
Axes of the slice: x: 4, y: 4, z: 8 (z_hi: 4, z_lo: 2; z = z_hi * 2 + z_lo), core: 2. Of those that a mesh axis runs over, the one named last changes fastest.
Arguments:
- activations: bfloat16 [1024, 2304], P('shard'), may hold values from -6 to 6
- encoder: bfloat16 [2304, 131072], P(None, ('band', 'shard')), may hold values from -0.125 to 0.125
- encoder_bias: float32 [131072], P(('band', 'shard')), may hold values from -1 to -0.25
- decoder: bfloat16 [131072, 2304], P(('band', 'shard')), may hold values from -0.125 to 0.125
Outputs:
- losses: float32 [16], replicated
- encoder_grad: bfloat16 [2304, 131072], P(None, ('band', 'shard'))
- decoder_grad: bfloat16 [131072, 2304], P(('band', 'shard'))
All inputs are finite; a program needn't handle non-finite values.
Results may differ from a plain program's by a relative error of at most 0.006.
Values may be sent and summed in bfloat16 or wider, within the bound.
No kernel may reach another device: no remote copies, remote signals or barrier semaphores. Data moves between devices by JAX's collectives and lax.ppermute only.
A program may use at most 128 MiB of HBM per device.

v0:
```python
import jax
import jax.numpy as jnp
from jax import lax
from jax.sharding import PartitionSpec as P


def over_pieces(value, axis):
    pieces = lax.all_gather(value, axis)
    return pieces.sum(axis=0)


def on_device(activations, encoder, encoder_bias, decoder):
    band_count = lax.axis_size("band")
    local_count = activations.shape[0]
    divisor = local_count * lax.axis_size("shard") * activations.shape[1]
    gathered = lax.all_gather(activations, "shard", axis=0, tiled=True)
    preact = jnp.dot(gathered, encoder, preferred_element_type=jnp.float32) + encoder_bias
    linear = jnp.maximum(preact, 0.0)
    active = (linear * linear).astype(jnp.bfloat16)
    act_rows = active
    band_part = lax.psum_scatter(
        jnp.dot(act_rows, decoder, preferred_element_type=jnp.float32),
        "shard",
        scatter_dimension=0,
        tiled=True,
    )
    local_rows = activations.astype(jnp.float32)
    stacked = lax.all_gather(band_part[None], "band", axis=0, tiled=True)
    prefix_recon = jnp.cumsum(stacked, axis=0)
    errors_all = local_rows[None] - prefix_recon
    losses = over_pieces(jnp.sum(errors_all * errors_all, axis=(1, 2)), "shard") / divisor
    tail_sums = jnp.flip(jnp.cumsum(jnp.flip(errors_all, 0), axis=0), 0)
    suffix = lax.dynamic_index_in_dim(tail_sums, lax.axis_index("band"), 0, keepdims=False)
    upstream = (-suffix / band_count).astype(jnp.bfloat16)
    shard_rows = lax.all_gather(upstream, "shard", axis=0, tiled=True)
    act_block = jnp.einsum("rd,ld->rl", shard_rows, decoder, preferred_element_type=jnp.float32)
    act_grads = act_block
    act_rows = active
    dec_grads = jnp.einsum("rl,rd->ld", act_rows, shard_rows, preferred_element_type=jnp.float32)
    act_grads, dec_grads = (act_grads, dec_grads)
    pre_grads = (2.0 * linear * act_grads).astype(jnp.bfloat16)
    encoder_grad = jnp.einsum(
        "rd,rl->dl", gathered, pre_grads, preferred_element_type=jnp.float32
    ).astype(jnp.bfloat16)
    return (losses, encoder_grad, dec_grads.astype(jnp.bfloat16))


def solution(mesh):
    return jax.shard_map(
        on_device,
        mesh=mesh,
        in_specs=(
            P("shard", None),
            P(None, ("band", "shard")),
            P(("band", "shard")),
            P(("band", "shard"), None),
        ),
        out_specs=(P(), P(None, ("band", "shard")), P(("band", "shard"), None)),
        check_vma=False,
    )
```

profile of v0, /device:TPU:35, one launch (start us, length us, event | category | flops | bytes accessed | tf_op | source)
XLA Modules:
  0.0 439.7 jit_solution(9953187625067713702)
XLA Ops:
  7.2 0.0 copy-start
  7.2 0.0 all-gather.7.cloned.1.call-start
  7.2 0.7 all-gather.7.cloned.1.call-update
  7.9 0.0 copy-start.2
  7.9 0.0 reduce-scatter.2.cloned.1.call-start
  8.0 87.1 %all-gather.7.cloned.1.call-done = bf16[1024,2304]{1,0:T(8,128)(2,1)} async-done(((bf16[64,2304]{1,0:T(8,128)(2,1)}), bf16[1024,2304]{1,0:T(8,128)(2,1)}) %all-gather.7.cloned.1.call-update) | async-done | bytes 4718608 | tf_op jit(solution)/shard_map/all_gather | solution.py:16
  95.1 5.2 %fusion.18 = f32[1024,512]{1,0:T(8,128)S(1)} fusion(bf16[1024,2304]{1,0:T(8,128)(2,1)} %all-gather.7.cloned.1.call-done, bf16[2304,512]{1,0:T(8,128)(2,1)} %param.5), kind=kOutput, calls=%fused_computation.20 | convolution fusion | flops 2415919104 | bytes 9175040 | tf_op jit(solution)/shard_map/dot_general | solution.py:17
  100.3 1.4 copy-done.4
  101.7 0.0 copy-done
  101.7 5.0 %fusion.12 = f32[1024,2304]{1,0:T(8,128)} fusion(bf16[512,2304]{1,0:T(8,128)(2,1)S(1)} %copy-done, f32[1024,512]{1,0:T(8,128)S(1)} %fusion.18, f32[512]{0:T(512)S(1)} %copy-done.2), kind=kOutput, calls=%fused_computation.13 | convolution fusion | flops 2418016256 | bytes 13895680 | tf_op jit(solution)/shard_map/dot_general | solution.py:22
  106.7 0.0 reduce-scatter.2.cloned.1.call-update
  106.7 0.0 all-gather.9.cloned.1.call-start
  106.8 127.4 %reduce-scatter.2.cloned.1.call-done = f32[64,2304]{1,0:T(8,128)} async-done(((f32[1024,2304]{1,0:T(8,128)}), f32[64,2304]{1,0:T(8,128)}) %reduce-scatter.2.cloned.1.call-update) | async-done | bytes 589840 | tf_op jit(solution)/shard_map/reduce_scatter | solution.py:21
  234.2 0.0 all-gather.9.cloned.1.call-update
  234.2 0.0 all-gather.11.cloned.1.call-start
  234.2 0.0 copy-done.1
  234.3 61.3 %all-gather.9.cloned.1.call-done = f32[1024,2304]{1,0:T(8,128)} async-done(((f32[64,2304]{1,0:T(8,128)}), f32[1024,2304]{1,0:T(8,128)}) %all-gather.9.cloned.1.call-update) | async-done | bytes 9437200 | tf_op jit(solution)/shard_map/all_gather | solution.py:28
  295.6 7.3 %multiply_reduce_fusion = (f32[16]{0:T(128)S(1)}, f32[16,64,2304]{2,1,0:T(8,128)}) fusion(f32[16,64,2304]{2,1,0:T(8,128)} %bitcast.22, f32[64,2304]{1,0:T(8,128)S(1)} %convert_element_type.24), kind=kOutput, calls=%fused_computation | output fusion | flops 42467312 | bytes 19464256 | tf_op jit(solution)/shard_map/jit(cumsum)/reduce_window_sum | solution.py:29
  302.9 8.2 %rev.7 = f32[16,64,2304]{2,1,0:T(8,128)} reverse(f32[16,64,2304]{2,1,0:T(8,128)} %get-tuple-element.10), dimensions={0} | reverse | bytes 18874368 | tf_op jit(solution)/shard_map/jit(_flip)/rev | solution.py:32
  311.2 6.6 %fusion.17 = f32[16,64,2304]{2,1,0:T(8,128)} fusion(f32[16,64,2304]{2,1,0:T(8,128)} %rev.7), kind=kOutput, calls=%fused_computation.19 | output fusion | flops 35389440 | bytes 18874368 | tf_op jit(solution)/shard_map/jit(cumsum)/reduce_window_sum | solution.py:32
  317.8 8.2 %rev.8 = f32[16,64,2304]{2,1,0:T(8,128)} reverse(f32[16,64,2304]{2,1,0:T(8,128)} %fusion.17), dimensions={0} | reverse | bytes 18874368 | tf_op jit(solution)/shard_map/jit(_flip)/rev | solution.py:32
  326.0 1.8 multiply_convert_fusion.2
  327.8 0.0 all-gather.11.cloned.1.call-update
  327.9 0.6 dynamic-slice
  329.1 0.2 dynamic-update-slice
  329.4 33.6 %all-reduce = f32[256]{0:T(256)S(1)} all-reduce(f32[256]{0:T(256)S(1)} %dynamic-update-slice), channel_id=3, replica_groups=mesh['band'=16,'shard'=16] {'shard'}, use_global_device_ids=true, to_apply=%add | all-reduce | flops 256 | bytes 2048
  363.0 0.1 reshape.13
  363.1 0.5 broadcast_multiply_fusion
  363.6 47.0 %all-gather.11.cloned.1.call-done = bf16[1,1024,2304]{2,1,0:T(8,128)(2,1)} async-done(((bf16[1,64,2304]{2,1,0:T(8,128)(2,1)}), bf16[1,1024,2304]{2,1,0:T(8,128)(2,1)}) %all-gather.11.cloned.1.call-update) | async-done | bytes 4718608 | tf_op jit(solution)/shard_map/all_gather | solution.py:35
  410.6 11.2 %fusion.7 = bf16[2304,512]{0,1:T(8,128)(2,1)} fusion(bf16[1024,2304]{1,0:T(8,128)(2,1)} %all-gather.7.cloned.1.call-done, f32[1024,512]{1,0:T(8,128)} %copy-done.4, bf16[512,2304]{1,0:T(8,128)(2,1)S(1)} %copy-done, bf16[1,1024,2304]{2,1,0:T(8,128)(2,1)} %all-gather.11.cloned.1.call-done, f32[512]{0:T(512)S(1)} %copy-done.2), kind=kOutput, calls=%fused_computation.8 | convolution fusion | flops 4835639296 | bytes 16254976 | tf_op jit(solution)/shard_map/rd,rl->dl/dot_general | solution.py:42
  421.8 4.3 copy.8
  426.1 7.1 %fusion.4 = bf16[512,2304]{1,0:T(8,128)(2,1)} fusion(bf16[1,1024,2304]{2,1,0:T(8,128)(2,1)} %all-gather.11.cloned.1.call-done, f32[1024,512]{1,0:T(8,128)} %copy-done.4, f32[512]{0:T(512)S(1)} %copy-done.2), kind=kOutput, calls=%fused_computation.6 | convolution fusion | flops 2419195904 | bytes 9177088 | tf_op jit(solution)/shard_map/rl,rd->ld/dot_general | solution.py:39
  (8 shorter events, 0.1 us)
Async XLA Ops:
  7.2 94.5 %copy-start = (bf16[512,2304]{1,0:T(8,128)(2,1)S(1)}, bf16[512,2304]{1,0:T(8,128)(2,1)}, u32[]{:S(2)}) copy-start(bf16[512,2304]{1,0:T(8,128)(2,1)} %param.7) | copy-start | bytes 7077892
  7.2 87.9 %all-gather.7.cloned.1.call-start = ((), (), s32[]{:S(2)}) async-start(), calls=%async_computation.1 | async-start | bytes 5013504 | tf_op jit(solution)/shard_map/all_gather | solution.py:16
  7.9 93.7 %copy-start.2 = (f32[512]{0:T(512)S(1)}, f32[512]{0:T(512)}, u32[]{:S(2)}) copy-start(f32[512]{0:T(512)} %param.6) | copy-start | bytes 6148
  7.9 226.3 %reduce-scatter.2.cloned.1.call-start = ((), (), s32[]{:S(2)}) async-start(), calls=%async_computation.2 | async-start | bytes 10027008 | tf_op jit(solution)/shard_map/reduce_scatter | solution.py:21
  100.3 1.4 copy-start.4
  106.7 127.6 %copy-start.1 = (bf16[64,2304]{1,0:T(8,128)(2,1)S(1)}, bf16[64,2304]{1,0:T(8,128)(2,1)}, u32[]{:S(2)}) copy-start(bf16[64,2304]{1,0:T(8,128)(2,1)} %param.4) | copy-start | bytes 884740
  106.7 188.9 %all-gather.9.cloned.1.call-start = ((), (), s32[]{:S(2)}) async-start(), calls=%async_computation.3 | async-start | bytes 10027008 | tf_op jit(solution)/shard_map/all_gather | solution.py:28
  234.2 176.4 %all-gather.11.cloned.1.call-start = ((), (), s32[]{:S(2)}) async-start(), calls=%async_computation.4 | async-start | bytes 5013504 | tf_op jit(solution)/shard_map/all_gather | solution.py:35
  317.8 10.1 %copy-start.3 = (u32[256]{0:T(256)S(1)}, u32[256]{0:T(256)}, u32[]{:S(2)}) copy-start(u32[256]{0:T(256)} %constant.28) | copy-start | bytes 3076
Sparse Core Ops, SparseCore 0:
  10.4 84.6 all-gather.6
  106.8 127.2 reduce-scatter.1
  236.0 59.5 all-gather.8
  328.0 82.5 all-gather.10
where the time goes:
time: 440 us
  waiting for transfers between devices  324 us (74%)
  blocking collectives  33.6 us (8%)
  matrix products  28.5 us (6%)
  local copies, waits for them, and re-layouts  23.1 us (5%)
  other arithmetic  16.3 us (4%)
  between operations  14.5 us (3%)
    reduce_scatter x1, waiting for transfers between devices, on_device(): lax.psum_scatter(jnp.dot(act_rows, decoder, preferred_element_type=jnp.fl...  127 us
    all_gather x1, waiting for transfers between devices, on_device(): gathered = lax.all_gather(activations, 'shard', axis=0, tiled=True)  87.1 us
    all_gather x1, waiting for transfers between devices, on_device(): stacked = lax.all_gather(band_part[None], 'band', axis=0, tiled=True)  61.3 us
    all_gather x1, waiting for transfers between devices, on_device(): shard_rows = lax.all_gather(upstream, 'shard', axis=0, tiled=True)  47 us
    unnamed x1, blocking collectives  33.6 us
    rev x2, local copies, waits for them, and re-layouts, on_device(): tail_sums = jnp.flip(jnp.cumsum(jnp.flip(errors_all, 0), axis=0), 0)  16.5 us
    dot_general x1, matrix products, on_device(): jnp.einsum('rd,rl->dl', gathered, pre_grads, preferred_element_type=jnp.f...  11.2 us
  transfers between devices with their start and end apart: 4, of which 4 were waited for; matrix products, arithmetic and copies ran while one was open for 0% of the time, Pallas kernels for 0%

commit v1 on v0

--- a/solution.py
+++ b/solution.py
@@ -2,6 +2,16 @@
 import jax.numpy as jnp
 from jax import lax
 from jax.sharding import PartitionSpec as P
+
+
+def wait_zones(page):
+    inter = jnp.concatenate(
+        lax.all_to_all(
+            jnp.stack([page for _ in range(lax.axis_size("shard"))], axis=0), "shard", 0, 0
+        ),
+        axis=0,
+    )
+    return inter
 
 
 def over_pieces(value, axis):
@@ -32,7 +42,7 @@
     tail_sums = jnp.flip(jnp.cumsum(jnp.flip(errors_all, 0), axis=0), 0)
     suffix = lax.dynamic_index_in_dim(tail_sums, lax.axis_index("band"), 0, keepdims=False)
     upstream = (-suffix / band_count).astype(jnp.bfloat16)
-    shard_rows = lax.all_gather(upstream, "shard", axis=0, tiled=True)
+    shard_rows = wait_zones(upstream)
     act_block = jnp.einsum("rd,ld->rl", shard_rows, decoder, preferred_element_type=jnp.float32)
     act_grads = act_block
     act_rows = active

time: 440 us -> 512 us (1.16)
  the two profiles are of different devices: /device:TPU:35 before, /device:TPU:58 now
where the time goes in v1:
time: 512 us; the launch traced here: 511 us
  waiting for transfers between devices  275 us (54%)
  blocking collectives  143 us (28%)
  matrix products  28.5 us (6%)
  local copies, waits for them, and re-layouts  25.6 us (5%)
  other arithmetic  15.5 us (3%)
  between operations  14.5 us (3%)
  starting transfers between devices  9.97 us (2%)
    unnamed x1, blocking collectives  143 us
    reduce_scatter x1, waiting for transfers between devices, on_device(): lax.psum_scatter(jnp.dot(act_rows, decoder, preferred_element_type=jnp.fl...  128 us
    all_gather x1, waiting for transfers between devices, on_device(): gathered = lax.all_gather(activations, 'shard', axis=0, tiled=True)  86.8 us
    all_gather x1, waiting for transfers between devices, on_device(): stacked = lax.all_gather(band_part[None], 'band', axis=0, tiled=True)  59.7 us
    rev x2, local copies, waits for them, and re-layouts, on_device(): tail_sums = jnp.flip(jnp.cumsum(jnp.flip(errors_all, 0), axis=0), 0)  16.5 us
    dot_general x1, matrix products, on_device(): jnp.einsum('rd,rl->dl', gathered, pre_grads, preferred_element_type=jnp.f...  11.3 us
  transfers between devices with their start and end apart: 4, of which 3 were waited for; matrix products, arithmetic and copies ran while one was open for 0% of the time, Pallas kernels for 0%

profile of v1, /device:TPU:58, one launch (start us, length us, event | category | flops | bytes accessed | tf_op | source)
XLA Modules:
  0.0 511.5 jit_solution(18358435343366002475)
XLA Ops:
  7.2 0.0 copy-start
  7.2 0.0 all-gather.5.cloned.1.call-start
  7.2 0.7 all-gather.5.cloned.1.call-update
  7.9 0.0 copy-start.2
  7.9 0.0 reduce-scatter.2.cloned.1.call-start
  8.0 86.8 %all-gather.5.cloned.1.call-done = bf16[1024,2304]{1,0:T(8,128)(2,1)} async-done(((bf16[64,2304]{1,0:T(8,128)(2,1)}), bf16[1024,2304]{1,0:T(8,128)(2,1)}) %all-gather.5.cloned.1.call-update) | async-done | bytes 4718608 | tf_op jit(solution)/shard_map/all_gather | solution.py:26
  94.8 5.2 %fusion.8 = f32[1024,512]{1,0:T(8,128)S(1)} fusion(bf16[1024,2304]{1,0:T(8,128)(2,1)} %all-gather.5.cloned.1.call-done, bf16[2304,512]{1,0:T(8,128)(2,1)} %param.5), kind=kOutput, calls=%fused_computation.17 | convolution fusion | flops 2415919104 | bytes 9175040 | tf_op jit(solution)/shard_map/dot_general | solution.py:27
  99.9 0.0 copy-start.4
  99.9 1.3 copy-done.4
  101.3 0.0 copy-done
  101.3 5.0 fusion.2
  106.3 0.0 reduce-scatter.2.cloned.1.call-update
  106.3 0.0 all-gather.7.cloned.1.call-start
  106.4 127.7 %reduce-scatter.2.cloned.1.call-done = f32[64,2304]{1,0:T(8,128)} async-done(((f32[1024,2304]{1,0:T(8,128)}), f32[64,2304]{1,0:T(8,128)}) %reduce-scatter.2.cloned.1.call-update) | async-done | bytes 589840 | tf_op jit(solution)/shard_map/reduce_scatter | solution.py:31
  234.0 0.0 all-gather.7.cloned.1.call-update
  234.1 59.7 %all-gather.7.cloned.1.call-done = f32[1024,2304]{1,0:T(8,128)} async-done(((f32[64,2304]{1,0:T(8,128)}), f32[1024,2304]{1,0:T(8,128)}) %all-gather.7.cloned.1.call-update) | async-done | bytes 9437200 | tf_op jit(solution)/shard_map/all_gather | solution.py:38
  293.8 7.3 %multiply_reduce_fusion = (f32[16]{0:T(128)S(1)}, f32[16,64,2304]{2,1,0:T(8,128)}) fusion(f32[16,64,2304]{2,1,0:T(8,128)} %bitcast.16, f32[64,2304]{1,0:T(8,128)S(1)} %convert_element_type.22), kind=kOutput, calls=%fused_computation | output fusion | flops 42467312 | bytes 19464256 | tf_op jit(solution)/shard_map/jit(cumsum)/reduce_window_sum | solution.py:39
  301.1 8.2 %rev.7 = f32[16,64,2304]{2,1,0:T(8,128)} reverse(f32[16,64,2304]{2,1,0:T(8,128)} %get-tuple-element.10), dimensions={0} | reverse | bytes 18874368 | tf_op jit(solution)/shard_map/jit(_flip)/rev | solution.py:42
  309.3 6.5 %fusion.7 = f32[16,64,2304]{2,1,0:T(8,128)} fusion(f32[16,64,2304]{2,1,0:T(8,128)} %rev.7), kind=kOutput, calls=%fused_computation.16 | output fusion | flops 35389440 | bytes 18874368 | tf_op jit(solution)/shard_map/jit(cumsum)/reduce_window_sum | solution.py:42
  315.9 8.2 %rev.8 = f32[16,64,2304]{2,1,0:T(8,128)} reverse(f32[16,64,2304]{2,1,0:T(8,128)} %fusion.7), dimensions={0} | reverse | bytes 18874368 | tf_op jit(solution)/shard_map/jit(_flip)/rev | solution.py:42
  324.1 1.1 fusion.1
  325.2 2.6 stack.5
  327.8 9.9 %all-to-all-start = ((bf16[16,64,2304]{2,1,0:T(8,128)(2,1)}), bf16[16,64,2304]{2,1,0:T(8,128)(2,1)}, u32[]{:S(2)}, u32[]{:S(2)}) async-start(bf16[16,64,2304]{2,1,0:T(8,128)(2,1)} %stack.5), calls=%async_computation.1 | async-start | bytes 9437184 | tf_op jit(solution)/shard_map/all_to_all | solution.py:9
  337.7 0.6 dynamic-slice
  338.9 0.2 dynamic-update-slice
  339.2 142.5 %all-reduce = f32[256]{0:T(256)S(1)} all-reduce(f32[256]{0:T(256)S(1)} %dynamic-update-slice), channel_id=3, replica_groups=mesh['band'=16,'shard'=16] {'shard'}, use_global_device_ids=true, to_apply=%add | all-reduce | flops 256 | bytes 2048
  481.7 0.1 reshape.14
  481.8 0.5 broadcast_multiply_fusion
  482.3 0.0 all-to-all-done
  482.3 7.1 %convolution_convert_fusion = bf16[512,2304]{1,0:T(8,128)(2,1)} fusion(bf16[1024,2304]{1,0:T(8,128)(2,1)} %bitcast.3, f32[1024,512]{1,0:T(8,128)} %copy-done.4, f32[512]{0:T(512)S(1)} %copy-done.2), kind=kOutput, calls=%fused_computation.2 | convolution fusion | flops 2419195904 | bytes 9177088 | tf_op jit(solution)/shard_map/rl,rd->ld/dot_general | solution.py:49
  489.4 11.3 %fusion = bf16[2304,512]{0,1:T(8,128)(2,1)} fusion(bf16[1024,2304]{1,0:T(8,128)(2,1)} %all-gather.5.cloned.1.call-done, f32[1024,512]{1,0:T(8,128)} %copy-done.4, bf16[1024,2304]{1,0:T(8,128)(2,1)} %bitcast.3, bf16[512,2304]{1,0:T(8,128)(2,1)S(1)} %copy-done, f32[512]{0:T(512)S(1)} %copy-done.2), kind=kOutput, calls=%fused_computation.4 | convolution fusion | flops 4835639296 | bytes 16254976 | tf_op jit(solution)/shard_map/rd,rl->dl/dot_general | solution.py:52
  500.7 4.3 copy.8
  (8 shorter events, 0.1 us)
Async XLA Ops:
  7.2 94.1 %copy-start = (bf16[512,2304]{1,0:T(8,128)(2,1)S(1)}, bf16[512,2304]{1,0:T(8,128)(2,1)}, u32[]{:S(2)}) copy-start(bf16[512,2304]{1,0:T(8,128)(2,1)} %param.7) | copy-start | bytes 7077892
  7.2 87.6 %all-gather.5.cloned.1.call-start = ((), (), s32[]{:S(2)}) async-start(), calls=%async_computation.2 | async-start | bytes 5013504 | tf_op jit(solution)/shard_map/all_gather | solution.py:26
  7.9 93.3 %copy-start.2 = (f32[512]{0:T(512)S(1)}, f32[512]{0:T(512)}, u32[]{:S(2)}) copy-start(f32[512]{0:T(512)} %param.6) | copy-start | bytes 6148
  7.9 226.1 %reduce-scatter.2.cloned.1.call-start = ((), (), s32[]{:S(2)}) async-start(), calls=%async_computation.3 | async-start | bytes 10027008 | tf_op jit(solution)/shard_map/reduce_scatter | solution.py:31
  99.9 1.3 copy-start.4
  106.3 127.8 %copy-start.1 = (bf16[64,2304]{1,0:T(8,128)(2,1)S(1)}, bf16[64,2304]{1,0:T(8,128)(2,1)}, u32[]{:S(2)}) copy-start(bf16[64,2304]{1,0:T(8,128)(2,1)} %param.4) | copy-start | bytes 884740
  106.3 187.5 %all-gather.7.cloned.1.call-start = ((), (), s32[]{:S(2)}) async-start(), calls=%async_computation.4 | async-start | bytes 10027008 | tf_op jit(solution)/shard_map/all_gather | solution.py:38
  327.8 9.9 %copy-start.3 = (u32[256]{0:T(256)S(1)}, u32[256]{0:T(256)}, u32[]{:S(2)}) copy-start(u32[256]{0:T(256)} %constant.28) | copy-start | bytes 3076
  327.8 154.5 %all-to-all-start = ((bf16[16,64,2304]{2,1,0:T(8,128)(2,1)}), bf16[16,64,2304]{2,1,0:T(8,128)(2,1)}, u32[]{:S(2)}, u32[]{:S(2)}) async-start(bf16[16,64,2304]{2,1,0:T(8,128)(2,1)} %stack.5), calls=%async_computation.1 | async-start | bytes 9437184 | tf_op jit(solution)/shard_map/all_to_all | solution.py:9
Sparse Core Ops, SparseCore 0:
  10.4 84.3 all-gather.4
  106.4 127.5 reduce-scatter.1
  235.9 57.9 all-gather.6
